TPU v7x, 128 devices: a whole 4x4x4 slice. The times are simulated.
128 devices in a mesh: gx: 4 (over y), gy: 4 (over x_hi, core), gz: 8 (over z, x_lo).
Axes of the slice: x: 4 (x_hi: 2, x_lo: 2; x = x_hi * 2 + x_lo), y: 4, z: 4, core: 2. Of those that a mesh axis runs over, the one named last changes fastest.
Arguments:
- concentration: float32 [512, 512, 512], P('gz', 'gx', 'gy'), may hold values from -1 to 1
Outputs:
- concentration_next: float32 [512, 512, 512], P('gz', 'gx', 'gy')
All inputs are finite; a program needn't handle non-finite values.
Results may differ from a plain program's by a relative error of at most 0.00011.
Values sent between devices are 32-bit elements; how exact they have to be, the bound alone decides.
A program may use at most 192 MiB of HBM per device.

v0:
```python
import functools
import jax
import jax.numpy as jnp
from jax import lax
from jax.sharding import Mesh
from jax.sharding import PartitionSpec as P

GY = ("gy_0", "gy_1")
GZ = ("gz_0", "gz_1")
GX_GY_GZ = ("gx", "gy_0", "gy_1", "gz_0", "gz_1")
step_length = 0.2
stiffness = 0.25


def padded_2(x, sides, width):
    edges = {}
    for axis, dim in sides:
        count, length = (lax.axis_size(axis), x.shape[dim])
        up = [(i, (i + 1) % count) for i in range(count)]
        last = lax.slice_in_dim(x, length - width, length, axis=dim)
        leading = lax.slice_in_dim(x, 0, width, axis=dim)
        edges[dim] = (
            lax.ppermute(last, axis, up),
            lax.ppermute(leading, axis, [(b, a) for a, b in up]),
        )
    done = []
    for _, dim in sides:
        low, high = edges[dim]
        around = [(width, width) if d in done else (0, 0) for d in range(x.ndim)]
        x = jnp.concatenate([jnp.pad(low, around), x, jnp.pad(high, around)], axis=dim)
        done.append(dim)
    return x


def by_axis(x, axes):
    return functools.reduce(lax.psum, axes, x)


def hartley_table(length):
    indices = jnp.arange(length, dtype=jnp.int32)
    product = indices[:, None] * indices[None, :] % length
    angles = 2.0 * jnp.pi / length * product.astype(jnp.float32)
    return (jnp.cos(angles) + jnp.sin(angles)) / jnp.sqrt(float(length))


def wave_square(length):
    indices = jnp.arange(length, dtype=jnp.int32)
    folded = jnp.minimum(indices, length - indices).astype(jnp.float32)
    wave = 2.0 * jnp.pi / length * folded
    return wave * wave


def column_matmul(matrix, source):
    flat_columns = source.reshape(source.shape[0], -1)
    mapped = jnp.dot(
        matrix, flat_columns, precision=lax.Precision.HIGHEST, preferred_element_type=jnp.float32
    )
    return mapped.reshape(source.shape)


def plane_pass(planes, hartley_x, hartley_y):
    mapped = jnp.einsum("ij,rjy->riy", hartley_x, planes, precision=lax.Precision.HIGHEST)
    flat_planes = mapped.reshape(-1, planes.shape[2])
    mapped = jnp.dot(
        flat_planes,
        hartley_y.T,
        precision=lax.Precision.HIGHEST,
        preferred_element_type=jnp.float32,
    )
    return mapped.reshape(planes.shape)


def face_terms(padded_pot, padded_mob, axis_number):
    length = padded_pot.shape[axis_number]
    lower_pot = lax.slice_in_dim(padded_pot, 0, length - 1, axis=axis_number)
    upper_pot = lax.slice_in_dim(padded_pot, 1, length, axis=axis_number)
    lower_mob = lax.slice_in_dim(padded_mob, 0, length - 1, axis=axis_number)
    upper_mob = lax.slice_in_dim(padded_mob, 1, length, axis=axis_number)
    flux = 0.5 * (lower_mob + upper_mob) * (upper_pot - lower_pot)
    count = flux.shape[axis_number]
    return lax.slice_in_dim(flux, 1, count, axis=axis_number) - lax.slice_in_dim(
        flux, 0, count - 1, axis=axis_number
    )


def solve_planes(planes, hartley_x, hartley_y, local_z, wave_x, wave_y, mean_mobility):
    planes = plane_pass(planes, hartley_x, hartley_y)
    wave_sum = local_z[:, None, None] + wave_x[None, :, None] + wave_y[None, None, :]
    planes = planes / (1.0 + step_length * stiffness * mean_mobility * wave_sum * wave_sum)
    return plane_pass(planes, hartley_x, hartley_y)


def local(concentration):
    block_z, block_x, block_y = concentration.shape
    groups_x = lax.axis_size("gx")
    groups_y = lax.axis_size(GY)
    groups_z = lax.axis_size(GZ)
    whole_z = block_z * groups_z
    whole_x = block_x * groups_x
    whole_y = block_y * groups_y
    hartley_z = hartley_table(whole_z)
    hartley_x = hartley_table(whole_x)
    hartley_y = hartley_table(whole_y)
    padded = padded_2(concentration, (("gx", 1), (GY, 2), (GZ, 0)), 1)
    padded_pot = padded * padded * padded - padded
    padded_mob = 1.05 - padded * padded
    mobility = padded_mob[1:-1, 1:-1, 1:-1]
    mobility_sum = by_axis(jnp.sum(mobility), GX_GY_GZ)
    mean_mobility = mobility_sum / (whole_x * whole_y * whole_z)
    divergence = face_terms(padded_pot[:, 1:-1, 1:-1], padded_mob[:, 1:-1, 1:-1], 0)
    divergence = divergence + face_terms(padded_pot[1:-1, :, 1:-1], padded_mob[1:-1, :, 1:-1], 1)
    divergence = divergence + face_terms(padded_pot[1:-1, 1:-1, :], padded_mob[1:-1, 1:-1, :], 2)
    update = concentration + step_length * divergence
    wave_z = wave_square(whole_z)
    wave_x = wave_square(whole_x)
    wave_y = wave_square(whole_y)
    devices = groups_x * groups_y * groups_z
    rows_each = whole_z // devices
    slim_x = block_x // groups_z
    member = (lax.axis_index("gx") * groups_y + lax.axis_index(GY)) * groups_z + lax.axis_index(GZ)
    pencil = lax.all_to_all(update, GZ, split_axis=1, concat_axis=0, tiled=True)
    pencil = column_matmul(hartley_z, pencil)
    outgoing = pencil.reshape(devices, rows_each, slim_x, block_y)
    received = lax.all_to_all(outgoing, GX_GY_GZ, split_axis=0, concat_axis=0, tiled=True)
    planes = received.reshape(groups_x, groups_y, groups_z, rows_each, slim_x, block_y)
    planes = planes.transpose(3, 0, 2, 4, 1, 5).reshape(rows_each, whole_x, whole_y)
    local_z = lax.dynamic_slice_in_dim(wave_z, member * rows_each, rows_each, 0)
    planes = solve_planes(planes, hartley_x, hartley_y, local_z, wave_x, wave_y, mean_mobility)
    returning = planes.reshape(rows_each, groups_x, groups_z, slim_x, groups_y, block_y)
    returning = returning.transpose(1, 4, 2, 0, 3, 5).reshape(devices, rows_each, slim_x, block_y)
    arrived = lax.all_to_all(returning, GX_GY_GZ, split_axis=0, concat_axis=0, tiled=True)
    pencil = column_matmul(hartley_z, arrived.reshape(whole_z, slim_x, block_y))
    return lax.all_to_all(pencil, GZ, split_axis=0, concat_axis=1, tiled=True)


def solution(mesh):
    torus = Mesh(
        mesh.devices.reshape(mesh.shape["gx"], 2, 2, 4, 2), ("gx", "gy_0", "gy_1", "gz_0", "gz_1")
    )
    in_specs = (P(GZ, "gx", GY),)
    out_specs = P(GZ, "gx", GY)
    return jax.shard_map(local, mesh=torus, in_specs=in_specs, out_specs=out_specs, check_vma=False)
```

profile of v0, /device:TPU:0, one launch (start us, length us, event | category | flops | bytes accessed | tf_op | source)
XLA Modules:
  0.0 495.5 jit_solution(6628184515026197495)
XLA Ops:
  0.0 8.1 %fusion.113 = (f32[64,128,1]{2,1,0:T(8,128)}, f32[64,128,1]{2,1,0:T(8,128)}) fusion(f32[64,128,128]{2,1,0:T(8,128)} %param.1), kind=kLoop, calls=%fused_computation.146 | loop fusion | bytes 131072 | tf_op jit(solution)/shard_map/slice | solution.py:20
  42.2 12.8 %multiply_subtract_fusion.1 = (f32[66,130,130]{2,0,1:T(8,128)S(1)}, f32[66,130,130]{2,0,1:T(8,128)}) fusion(f32[1,128,128]{2,0,1:T(1,128)S(1)} %collective-permute-done.5, f32[64,128,1]{2,0,1:T(8,128)} %copy.38, f32[64,1,128]{2,0,1:T(8,128)S(1)} %collective-permute-done.3, f32[64,128,128]{2,0,1:T(8,128)} %copy-done.1, ...), kind=kLoop, calls=%fused_computation.3 | loop fusion | flops 27885000 | bytes 13379648 | tf_op jit(solution)/shard_map/sub | solution.py:106
  55.0 14.1 %fusion.6 = f32[65,128,128]{2,0,1:T(8,128)} fusion(f32[66,130,130]{2,0,1:T(8,128)} %get-tuple-element.6, f32[66,130,130]{2,0,1:T(8,128)S(1)} %get-tuple-element.5), kind=kLoop, calls=%fused_computation.21 | loop fusion | flops 4259840 | bytes 21299200 | tf_op jit(solution)/shard_map/mul | solution.py:79
  69.1 10.4 %fusion.8 = f32[64,129,128]{2,0,1:T(8,128)} fusion(f32[66,130,130]{2,0,1:T(8,128)} %get-tuple-element.6, f32[66,130,130]{2,0,1:T(8,128)S(1)} %get-tuple-element.5), kind=kLoop, calls=%fused_computation.25 | loop fusion | flops 4227072 | bytes 21135360 | tf_op jit(solution)/shard_map/mul | solution.py:79
  79.5 15.3 %fusion.4 = f32[64,128,129]{2,0,1:T(8,128)} fusion(f32[66,130,130]{2,0,1:T(8,128)} %get-tuple-element.6, f32[66,130,130]{2,0,1:T(8,128)S(1)} %get-tuple-element.5), kind=kLoop, calls=%fused_computation.16 | loop fusion | flops 4227072 | bytes 21135360 | tf_op jit(solution)/shard_map/mul | solution.py:79
  94.7 14.9 %fusion.16 = f32[64,128,128]{2,0,1:T(8,128)} fusion(f32[64,128,129]{2,0,1:T(8,128)} %fusion.4, f32[64,129,128]{2,0,1:T(8,128)} %fusion.8, f32[65,128,128]{2,0,1:T(8,128)} %fusion.6, f32[64,128,128]{2,1,0:T(8,128)} %param.1), kind=kLoop, calls=%fused_computation.37 | loop fusion | flops 7340032 | bytes 33554432 | tf_op jit(solution)/shard_map/add | solution.py:113
  114.2 48.1 %all-to-all-done = f32[64,128,128]{2,0,1:T(8,128)} async-done(((f32[64,128,128]{2,0,1:T(8,128)}), f32[64,128,128]{2,0,1:T(8,128)}, u32[]{:S(2)}, u32[]{:S(2)}) %all-to-all-start) | async-done | bytes 4194336 | tf_op jit(solution)/shard_map/all_to_all | solution.py:121
  170.9 5.8 %copy.21 = f32[2048,512]{1,0:T(8,128)} copy(f32[2048,512]{0,1:T(8,128)} %bitcast.74) | data formatting | bytes 8388608 | tf_op jit(solution)/shard_map/dot_general | solution.py:55
  176.7 13.2 %fusion.35 = f32[128,4,16,128]{3,0,2,1:T(8,128)S(1)} fusion(f32[16,128,512,1]{2,1,0,3:T(8,128)} %bitcast.72, s32[128,4]{0,1:T(4,128)S(1)} %multiply_add_fusion.1), kind=kOutput, calls=%fused_computation.69 | convolution fusion | flops 6446645248 | bytes 8390656 | tf_op jit(solution)/shard_map/dot_general | solution.py:55
  194.6 6.7 %all-to-all-start.1 = ((f32[128,4,16,128]{3,2,1,0:T(8,128)}), f32[128,4,16,128]{3,2,1,0:T(8,128)}, u32[]{:S(2)}, u32[]{:S(2)}) async-start(f32[128,4,16,128]{3,2,1,0:T(8,128)} %copy.22), calls=%async_computation.1 | async-start | bytes 8388608 | tf_op jit(solution)/shard_map/all_to_all | solution.py:124
  206.8 43.6 %psum.35 = f32[]{:T(128)} all-reduce(f32[]{:T(128)} %slice_reduce_fusion), channel_id=1, replica_groups=mesh['gx'=4,'gy_0'=2,'gy_1'=2,'gz_0'=4,'gz_1'=2] {'gx'}, use_global_device_ids=true, to_apply=%region_1.2 | all-reduce | flops 1 | bytes 8 | tf_op jit(solution)/shard_map/psum | solution.py:36
  250.3 7.0 %psum.36 = f32[]{:T(128)} all-reduce(f32[]{:T(128)} %psum.35), channel_id=1, replica_groups=mesh['gx'=4,'gy_0'=2,'gy_1'=2,'gz_0'=4,'gz_1'=2] {'gy_0'}, use_global_device_ids=true, to_apply=%region_2.3 | all-reduce | flops 1 | bytes 8 | tf_op jit(solution)/shard_map/psum | solution.py:36
  260.6 12.4 %psum.38 = f32[]{:T(128)} all-reduce(f32[]{:T(128)} %psum.37), channel_id=1, replica_groups=mesh['gx'=4,'gy_0'=2,'gy_1'=2,'gz_0'=4,'gz_1'=2] {'gz_0'}, use_global_device_ids=true, to_apply=%region_4.5 | all-reduce | flops 1 | bytes 8 | tf_op jit(solution)/shard_map/psum | solution.py:36
  273.0 5.5 %psum.39 = f32[]{:T(128)} all-reduce(f32[]{:T(128)} %psum.38), channel_id=1, replica_groups=mesh['gx'=4,'gy_0'=2,'gy_1'=2,'gz_0'=4,'gz_1'=2] {'gz_1'}, use_global_device_ids=true, to_apply=%region_5.6 | all-reduce | flops 1 | bytes 8 | tf_op jit(solution)/shard_map/psum | solution.py:36
  279.2 6.9 %copy.47 = f32[4,4,8,4,16,128]{5,1,4,2,0,3:T(4,128)} copy(f32[4,4,8,4,16,128]{5,4,3,2,1,0:T(8,128)} %bitcast.11) | data formatting | bytes 8388608 | tf_op jit(solution)/shard_map/reshape | solution.py:125
  286.1 5.5 %reshape.232 = f32[4,512,512]{2,1,0:T(8,128)} reshape(f32[4,4,8,16,4,128]{5,4,3,2,1,0:T(4,128)} %bitcast.75) | data formatting | bytes 8388608 | tf_op jit(solution)/shard_map/reshape | solution.py:126
  291.5 20.3 %fusion.41 = f32[4,512,512]{2,1,0:T(8,128)S(1)} fusion(f32[4,512,512]{2,1,0:T(8,128)} %reshape.232), kind=kOutput, calls=%fused_computation.75 | convolution fusion | flops 6446645248 | bytes 8388608 | tf_op jit(solution)/shard_map/ij,rjy->riy/dot_general | solution.py:62
  311.8 19.9 %fusion.18 = f32[4,512,512]{2,1,0:T(8,128)S(1)} fusion(f32[4,512,512]{2,1,0:T(8,128)S(1)} %fusion.41), kind=kOutput, calls=%fused_computation.41 | convolution fusion | flops 6446645248 | bytes 8388608 | tf_op jit(solution)/shard_map/dot_general | solution.py:64
  331.7 13.4 %fusion.12 = f32[4,512,512]{1,2,0:T(8,128)S(1)} fusion(f32[4,512,512]{2,1,0:T(8,128)S(1)} %fusion.18, f32[512]{0:T(512)S(1)} %fusion.80, f32[4,512]{1,0:T(4,128)S(1)} %broadcast_add_fusion, f32[]{:T(128)S(6)} %mul_shard_map.3), kind=kOutput, calls=%fused_computation.30 | convolution fusion | flops 6451888128 | bytes 8398852 | tf_op jit(solution)/shard_map/ij,rjy->riy/dot_general | solution.py:62
  345.1 11.1 %convolution_bitcast_fusion = f32[4,4,8,4,16,128]{5,4,1,2,0,3:T(8,128)S(1)} fusion(f32[4,4,8,16,512,1]{4,3,5,2,1,0:T(8,128)S(1)} %bitcast.80, s32[4,128]{1,0:T(4,128)S(1)} %multiply_add_fusion), kind=kOutput, calls=%fused_computation.45 | convolution fusion | flops 6446645248 | bytes 8390656 | tf_op jit(solution)/shard_map/dot_general | solution.py:64
  356.8 59.6 %all_to_all.43 = f32[128,4,16,128]{3,2,1,0:T(8,128)S(1)} all-to-all(f32[128,4,16,128]{3,2,1,0:T(8,128)S(1)} %bitcast.76), channel_id=1, replica_groups=mesh['gx'=4,'gy_0'=2,'gy_1'=2,'gz_0'=4,'gz_1'=2] {'gx','gy_0','gy_1','gz..., dimensions={0} | all-to-all | bytes 8388608 | tf_op jit(solution)/shard_map/all_to_all | solution.py:131
  420.4 5.5 %copy.27 = f32[2048,512]{1,0:T(8,128)} copy(f32[2048,512]{0,1:T(8,128)} %bitcast.78) | data formatting | bytes 8388608 | tf_op jit(solution)/shard_map/dot_general | solution.py:55
  425.9 13.2 %fusion.37 = f32[512,16,128]{2,0,1:T(8,128)S(1)} fusion(f32[16,128,512]{2,1,0:T(8,128)} %bitcast.71), kind=kOutput, calls=%fused_computation.71 | convolution fusion | flops 6446645248 | bytes 8388608 | tf_op jit(solution)/shard_map/dot_general | solution.py:55
  441.5 51.2 %all_to_all.44 = f32[512,16,128]{2,1,0:T(8,128)S(1)} all-to-all(f32[512,16,128]{2,1,0:T(8,128)S(1)} %copy.28), channel_id=1, replica_groups=mesh['gx'=4,'gy_0'=2,'gy_1'=2,'gz_0'=4,'gz_1'=2] {'gz_0','gz_1'}, dimensions={0} | all-to-all | bytes 8388608 | tf_op jit(solution)/shard_map/all_to_all | solution.py:133
  (39 shorter events, 70.1 us)
Async XLA Ops:
  10.9 20.5 %collective-permute-start.1 = (f32[64,128,1]{1,0,2:T(8,128)S(1)}, f32[64,128,1]{1,0,2:T(8,128)S(1)}, u32[]{:S(2)}, u32[]{:S(2)}) collective-permute-start(f32[64,128,1]{1,0,2:T(8,128)S(1)} %copy.35), channel_id=1, source_target_pairs={{0,8},{8,16},{16,24},{24,0},{1,9},{9,17},{17,25},{25,1},{2,10},{10... | collective-permute-start | bytes 98312 | tf_op jit(solution)/shard_map/ppermute | solution.py:23
  11.9 30.3 %collective-permute-start = (f32[1,128,128]{2,0,1:T(1,128)S(1)}, f32[1,128,128]{2,0,1:T(1,128)S(1)}, u32[]{:S(2)}, u32[]{:S(2)}) collective-permute-start(f32[1,128,128]{2,0,1:T(1,128)S(1)} %bitcast.82), channel_id=1, source_target_pairs={{0,1},{1,2},{2,3},{3,4},{4,5},{5,6},{6,7},{7,0},{8,9},{9,10},{10,1... | collective-permute-start | bytes 196616 | tf_op jit(solution)/shard_map/ppermute | solution.py:23
  13.6 28.6 %collective-permute-start.5 = (f32[1,128,128]{2,0,1:T(1,128)S(1)}, f32[1,128,128]{2,0,1:T(1,128)S(1)}, u32[]{:S(2)}, u32[]{:S(2)}) collective-permute-start(f32[1,128,128]{2,0,1:T(1,128)S(1)} %bitcast.81), channel_id=1, source_target_pairs={{1,0},{2,1},{3,2},{4,3},{5,4},{6,5},{7,6},{0,7},{9,8},{10,9},{11,1... | collective-permute-start | bytes 196616 | tf_op jit(solution)/shard_map/ppermute | solution.py:24
  21.7 1.9 copy-start.1
  23.7 18.5 %collective-permute-start.2 = (f32[64,1,128]{2,0,1:T(8,128)S(1)}, f32[64,1,128]{2,0,1:T(8,128)S(1)}, u32[]{:S(2)}, u32[]{:S(2)}) collective-permute-start(f32[64,1,128]{2,0,1:T(8,128)S(1)} %get-tuple-element.11), channel_id=1, source_target_pairs={{0,32},{32,64},{64,96},{96,0},{1,33},{33,65},{65,97},{97,1},{2,34}... | collective-permute-start | bytes 98312 | tf_op jit(solution)/shard_map/ppermute | solution.py:23
  28.1 9.7 %collective-permute-start.4 = (f32[64,128,1]{1,0,2:T(8,128)S(1)}, f32[64,128,1]{1,0,2:T(8,128)S(1)}, u32[]{:S(2)}, u32[]{:S(2)}) collective-permute-start(f32[64,128,1]{1,0,2:T(8,128)S(1)} %copy.36), channel_id=1, source_target_pairs={{8,0},{16,8},{24,16},{0,24},{9,1},{17,9},{25,17},{1,25},{10,2},{18... | collective-permute-start | bytes 98312 | tf_op jit(solution)/shard_map/ppermute | solution.py:24
  31.4 10.7 %collective-permute-start.3 = (f32[64,1,128]{2,0,1:T(8,128)S(1)}, f32[64,1,128]{2,0,1:T(8,128)S(1)}, u32[]{:S(2)}, u32[]{:S(2)}) collective-permute-start(f32[64,1,128]{2,0,1:T(8,128)S(1)} %get-tuple-element.12), channel_id=1, source_target_pairs={{32,0},{64,32},{96,64},{0,96},{33,1},{65,33},{97,65},{1,97},{34,2}... | collective-permute-start | bytes 98312 | tf_op jit(solution)/shard_map/ppermute | solution.py:24
  54.9 24.5 %copy-start = (f32[66,130,130]{2,0,1:T(8,128)}, f32[66,130,130]{2,0,1:T(8,128)S(1)}, u32[]{:S(2)}) copy-start(f32[66,130,130]{2,0,1:T(8,128)S(1)} %get-tuple-element.5) | copy-start | bytes 13384804
  109.7 52.7 %all-to-all-start = ((f32[64,128,128]{2,0,1:T(8,128)}), f32[64,128,128]{2,0,1:T(8,128)}, u32[]{:S(2)}, u32[]{:S(2)}) async-start(f32[64,128,128]{2,0,1:T(8,128)} %fusion.16), calls=%async_computation | async-start | bytes 8388608 | tf_op jit(solution)/shard_map/all_to_all | solution.py:121
  194.6 84.6 %all-to-all-start.1 = ((f32[128,4,16,128]{3,2,1,0:T(8,128)}), f32[128,4,16,128]{3,2,1,0:T(8,128)}, u32[]{:S(2)}, u32[]{:S(2)}) async-start(f32[128,4,16,128]{3,2,1,0:T(8,128)} %copy.22), calls=%async_computation.1 | async-start | bytes 8388608 | tf_op jit(solution)/shard_map/all_to_all | solution.py:124
where the time goes:
time: 502 us; the launch traced here: 496 us
  blocking collectives  182 us (36%)
  matrix products  91 us (18%)
  local copies, waits for them, and re-layouts  76.6 us (15%)
  other arithmetic  73 us (15%)
  waiting for transfers between devices  48.1 us (10%)
  starting transfers between devices  23.4 us (5%)
    psum x5, blocking collectives, by_axis(): return functools.reduce(lax.psum, axes, x)  71.7 us
    all_to_all x1, blocking collectives, local(): lax.all_to_all(returning, GX_GY_GZ, split_axis=0, concat_axis=0, tiled=True)  59.6 us
    all_to_all x1, blocking collectives, local(): return lax.all_to_all(pencil, GZ, split_axis=0, concat_axis=1, tiled=True)  51.2 us
    all_to_all x1, waiting for transfers between devices, local(): pencil = lax.all_to_all(update, GZ, split_axis=1, concat_axis=0, tiled=True)  48.1 us
    mul x3, other arithmetic, face_terms(): flux = 0.5 * (lower_mob + upper_mob) * (upper_pot - lower_pot)  39.8 us
    dot_general x2, matrix products, plane_pass(): jnp.einsum('ij,rjy->riy', hartley_x, planes, precision=lax.Precision.HIGH...  33.7 us
    dot_general x2, matrix products, plane_pass(): jnp.dot(flat_planes, hartley_y.T, precision=lax.Precision.HIGHEST, prefer...  31 us
    unnamed x11, local copies, waits for them, and re-layouts  29 us
  transfers between devices with their start and end apart: 8, of which 1 were waited for; matrix products, arithmetic and copies ran while one was open for 5% of the time, Pallas kernels for 0%

commit v1 on v0

--- a/solution.py
+++ b/solution.py
@@ -118,7 +118,9 @@
     rows_each = whole_z // devices
     slim_x = block_x // groups_z
     member = (lax.axis_index("gx") * groups_y + lax.axis_index(GY)) * groups_z + lax.axis_index(GZ)
-    pencil = lax.all_to_all(update, GZ, split_axis=1, concat_axis=0, tiled=True)
+    pencil = jnp.concatenate(
+        lax.all_to_all(jnp.stack(jnp.split(update, lax.axis_size(GZ), axis=1)), GZ, 0, 0), axis=0
+    )
     pencil = column_matmul(hartley_z, pencil)
     outgoing = pencil.reshape(devices, rows_each, slim_x, block_y)
     received = lax.all_to_all(outgoing, GX_GY_GZ, split_axis=0, concat_axis=0, tiled=True)

time: 502 us -> 507 us (level)
  other arithmetic: 73 us -> 84.2 us
    sub x0 -> x1, other arithmetic: none -> 11.5 us  [local(): padded_pot = padded * padded * padded - padded]
    another operation x0 -> x2, local copies, waits for them, and re-layouts: none -> 6.39 us  [the longest x1 5.56 us: column_matmul(): flat_columns = source.reshape(source.shape[0], -1)]
    dot_general x4 -> x3, local copies, waits for them, and re-layouts: 18.4 us -> 12.8 us  [column_matmul(): jnp.dot(matrix, flat_columns, precision=lax.Precision.HIGHEST, preferred_...]
    unnamed x11 -> x15, local copies, waits for them, and re-layouts: 29 us -> 26.9 us
  transfers between devices with their start and end apart: 8 -> 8, of which waited for: 1 -> 1; matrix products, arithmetic and copies ran while one was open for 5% -> 3% of each run, Pallas kernels for 0% -> 0%
where the time goes in v1:
time: 507 us; the launch traced here: 502 us
  blocking collectives  183 us (36%)
  matrix products  90.8 us (18%)
  other arithmetic  84.2 us (17%)
  local copies, waits for them, and re-layouts  71.8 us (14%)
  waiting for transfers between devices  48.2 us (10%)
  starting transfers between devices  23.4 us (5%)
    psum x5, blocking collectives, by_axis(): return functools.reduce(lax.psum, axes, x)  71.8 us
    all_to_all x1, blocking collectives, local(): lax.all_to_all(returning, GX_GY_GZ, split_axis=0, concat_axis=0, tiled=True)  59.6 us
    all_to_all x1, blocking collectives, local(): return lax.all_to_all(pencil, GZ, split_axis=0, concat_axis=1, tiled=True)  51.2 us
    all_to_all x1, waiting for transfers between devices, local(): lax.all_to_all(jnp.stack(jnp.split(update, lax.axis_size(GZ), axis=1)), G...  48.2 us
    mul x3, other arithmetic, face_terms(): flux = 0.5 * (lower_mob + upper_mob) * (upper_pot - lower_pot)  39.3 us
    dot_general x2, matrix products, plane_pass(): jnp.einsum('ij,rjy->riy', hartley_x, planes, precision=lax.Precision.HIGH...  33.2 us
    dot_general x2, matrix products, plane_pass(): jnp.dot(flat_planes, hartley_y.T, precision=lax.Precision.HIGHEST, prefer...  31.2 us
    unnamed x15, local copies, waits for them, and re-layouts  26.9 us
  transfers between devices with their start and end apart: 8, of which 1 were waited for; matrix products, arithmetic and copies ran while one was open for 3% of the time, Pallas kernels for 0%

profile of v1, /device:TPU:0, one launch (start us, length us, event | category | flops | bytes accessed | tf_op | source)
XLA Modules:
  0.0 502.0 jit_solution(17537794128075092280)
XLA Ops:
  0.0 8.1 %fusion.121 = (f32[64,128,1]{2,1,0:T(8,128)}, f32[64,128,1]{2,1,0:T(8,128)}) fusion(f32[64,128,128]{2,1,0:T(8,128)} %param.1), kind=kLoop, calls=%fused_computation.162 | loop fusion | bytes 131072 | tf_op jit(solution)/shard_map/slice | solution.py:20
  33.2 15.8 %multiply_subtract_fusion.1 = (f32[66,130,130]{2,1,0:T(8,128)S(1)}, f32[66,130,130]{2,1,0:T(8,128)}) fusion(f32[1,128,128]{2,1,0:T(8,128)S(1)} %collective-permute-done.5, f32[64,128,1]{2,1,0:T(8,128)} %copy.30, f32[64,1,128]{2,1,0:T(1,128)S(1)} %collective-permute-done.3, f32[64,128,128]{2,1,0:T(8,128)} %param.1, ...), kind=kLoop, calls=%fused_computation.3 | loop fusion | flops 25654200 | bytes 13379648 | tf_op jit(solution)/shard_map/sub | solution.py:106
  48.9 11.5 %multiply_subtract_fusion = f32[66,130,130]{2,1,0:T(8,128)} fusion(f32[66,130,130]{2,1,0:T(8,128)} %get-tuple-element.6), kind=kLoop, calls=%fused_computation.2 | loop fusion | flops 3346200 | bytes 8923200 | tf_op jit(solution)/shard_map/sub | solution.py:105
  60.4 9.9 %fusion.8 = f32[65,128,128]{2,1,0:T(8,128)} fusion(f32[66,130,130]{2,1,0:T(8,128)} %multiply_subtract_fusion, f32[66,130,130]{2,1,0:T(8,128)S(1)} %get-tuple-element.5), kind=kLoop, calls=%fused_computation.25 | loop fusion | flops 4259840 | bytes 21299200 | tf_op jit(solution)/shard_map/mul | solution.py:79
  70.4 13.4 %fusion.6 = f32[64,129,128]{2,1,0:T(8,128)} fusion(f32[66,130,130]{2,1,0:T(8,128)} %multiply_subtract_fusion, f32[66,130,130]{2,1,0:T(8,128)S(1)} %get-tuple-element.5), kind=kLoop, calls=%fused_computation.21 | loop fusion | flops 4227072 | bytes 21135360 | tf_op jit(solution)/shard_map/mul | solution.py:79
  83.7 16.0 %fusion.4 = f32[64,128,129]{2,1,0:T(8,128)} fusion(f32[66,130,130]{2,1,0:T(8,128)} %multiply_subtract_fusion, f32[66,130,130]{2,1,0:T(8,128)S(1)} %get-tuple-element.5), kind=kLoop, calls=%fused_computation.16 | loop fusion | flops 4227072 | bytes 21135360 | tf_op jit(solution)/shard_map/mul | solution.py:79
  99.7 12.3 %fusion.16 = f32[64,128,128]{2,1,0:T(8,128)S(1)} fusion(f32[64,128,128]{2,1,0:T(8,128)} %param.1, f32[64,128,129]{2,1,0:T(8,128)} %fusion.4, f32[64,129,128]{2,1,0:T(8,128)} %fusion.6, f32[65,128,128]{2,1,0:T(8,128)} %fusion.8), kind=kLoop, calls=%fused_computation.37 | loop fusion | flops 7340032 | bytes 33554432 | tf_op jit(solution)/shard_map/add | solution.py:113
  123.3 48.2 %all-to-all-done = f32[8,64,16,128]{3,2,1,0:T(8,128)} async-done(((f32[8,64,16,128]{3,2,1,0:T(8,128)}), f32[8,64,16,128]{3,2,1,0:T(8,128)}, u32[]{:S(2)}, u32[]{:S(2)}) %all-to-all-start) | async-done | bytes 4194336 | tf_op jit(solution)/shard_map/all_to_all | solution.py:122
  171.5 6.2 %copy.37 = f32[64,8,16,128]{3,1,2,0:T(8,128)} copy(f32[64,8,16,128]{3,2,1,0:T(8,128)} %bitcast.42) | data formatting | bytes 8388608
  177.7 5.6 %copy.13 = f32[512,2048]{0,1:T(8,128)} copy(f32[512,2048]{1,0:T(8,128)} %bitcast.100) | data formatting | bytes 8388608 | tf_op jit(solution)/shard_map/reshape;reshape | solution.py:54
  183.2 13.2 %fusion.35 = f32[128,4,16,128]{3,0,2,1:T(8,128)S(1)} fusion(f32[16,128,512,1]{2,1,0,3:T(8,128)} %bitcast.99, s32[128,4]{0,1:T(4,128)S(1)} %multiply_add_fusion.1), kind=kOutput, calls=%fused_computation.69 | convolution fusion | flops 6446645248 | bytes 8390656 | tf_op jit(solution)/shard_map/dot_general | solution.py:55
  201.3 6.6 %all-to-all-start.1 = ((f32[128,4,16,128]{3,2,1,0:T(8,128)}), f32[128,4,16,128]{3,2,1,0:T(8,128)}, u32[]{:S(2)}, u32[]{:S(2)}) async-start(f32[128,4,16,128]{3,2,1,0:T(8,128)} %copy.14), calls=%async_computation.1 | async-start | bytes 8388608 | tf_op jit(solution)/shard_map/all_to_all | solution.py:126
  213.2 43.7 %psum.35 = f32[]{:T(128)} all-reduce(f32[]{:T(128)} %slice_reduce_fusion), channel_id=1, replica_groups=mesh['gx'=4,'gy_0'=2,'gy_1'=2,'gz_0'=4,'gz_1'=2] {'gx'}, use_global_device_ids=true, to_apply=%region_1.2 | all-reduce | flops 1 | bytes 8 | tf_op jit(solution)/shard_map/psum | solution.py:36
  256.9 7.0 %psum.36 = f32[]{:T(128)} all-reduce(f32[]{:T(128)} %psum.35), channel_id=1, replica_groups=mesh['gx'=4,'gy_0'=2,'gy_1'=2,'gz_0'=4,'gz_1'=2] {'gy_0'}, use_global_device_ids=true, to_apply=%region_2.3 | all-reduce | flops 1 | bytes 8 | tf_op jit(solution)/shard_map/psum | solution.py:36
  267.2 12.4 %psum.38 = f32[]{:T(128)} all-reduce(f32[]{:T(128)} %psum.37), channel_id=1, replica_groups=mesh['gx'=4,'gy_0'=2,'gy_1'=2,'gz_0'=4,'gz_1'=2] {'gz_0'}, use_global_device_ids=true, to_apply=%region_4.5 | all-reduce | flops 1 | bytes 8 | tf_op jit(solution)/shard_map/psum | solution.py:36
  285.7 6.9 %copy.38 = f32[4,4,8,4,16,128]{5,1,4,2,0,3:T(4,128)} copy(f32[4,4,8,4,16,128]{5,4,3,2,1,0:T(8,128)} %bitcast.15) | data formatting | bytes 8388608 | tf_op jit(solution)/shard_map/reshape | solution.py:127
  298.1 20.0 %fusion.41 = f32[4,512,512]{2,1,0:T(8,128)S(1)} fusion(f32[4,512,512]{2,1,0:T(8,128)} %reshape.227), kind=kOutput, calls=%fused_computation.75 | convolution fusion | flops 6446645248 | bytes 8388608 | tf_op jit(solution)/shard_map/ij,rjy->riy/dot_general | solution.py:62
  318.1 20.1 %fusion.18 = f32[4,512,512]{2,1,0:T(8,128)S(1)} fusion(f32[4,512,512]{2,1,0:T(8,128)S(1)} %fusion.41), kind=kOutput, calls=%fused_computation.41 | convolution fusion | flops 6446645248 | bytes 8388608 | tf_op jit(solution)/shard_map/dot_general | solution.py:64
  338.3 13.2 %fusion.12 = f32[4,512,512]{1,2,0:T(8,128)S(1)} fusion(f32[4,512,512]{2,1,0:T(8,128)S(1)} %fusion.18, f32[512]{0:T(512)S(1)} %fusion.88, f32[4,512]{1,0:T(4,128)S(1)} %broadcast_add_fusion, f32[]{:T(128)S(6)} %mul_shard_map.3), kind=kOutput, calls=%fused_computation.30 | convolution fusion | flops 6451888128 | bytes 8398852 | tf_op jit(solution)/shard_map/ij,rjy->riy/dot_general | solution.py:62
  351.5 11.1 %convolution_bitcast_fusion = f32[4,4,8,4,16,128]{5,4,1,2,0,3:T(8,128)S(1)} fusion(f32[4,4,8,16,512,1]{4,3,5,2,1,0:T(8,128)S(1)} %bitcast.106, s32[4,128]{1,0:T(4,128)S(1)} %multiply_add_fusion), kind=kOutput, calls=%fused_computation.45 | convolution fusion | flops 6446645248 | bytes 8390656 | tf_op jit(solution)/shard_map/dot_general | solution.py:64
  363.2 59.6 %all_to_all.33 = f32[128,4,16,128]{3,2,1,0:T(8,128)S(1)} all-to-all(f32[128,4,16,128]{3,2,1,0:T(8,128)S(1)} %bitcast.102), channel_id=1, replica_groups=mesh['gx'=4,'gy_0'=2,'gy_1'=2,'gz_0'=4,'gz_1'=2] {'gx','gy_0','gy_1','gz..., dimensions={0} | all-to-all | bytes 8388608 | tf_op jit(solution)/shard_map/all_to_all | solution.py:133
  426.8 5.5 %copy.19 = f32[2048,512]{1,0:T(8,128)} copy(f32[2048,512]{0,1:T(8,128)} %bitcast.104) | data formatting | bytes 8388608 | tf_op jit(solution)/shard_map/dot_general | solution.py:55
  432.3 13.2 %fusion.37 = f32[512,16,128]{2,0,1:T(8,128)S(1)} fusion(f32[16,128,512]{2,1,0:T(8,128)} %bitcast.98), kind=kOutput, calls=%fused_computation.71 | convolution fusion | flops 6446645248 | bytes 8388608 | tf_op jit(solution)/shard_map/dot_general | solution.py:55
  447.9 51.2 %all_to_all.34 = f32[512,16,128]{2,1,0:T(8,128)S(1)} all-to-all(f32[512,16,128]{2,1,0:T(8,128)S(1)} %copy.20), channel_id=1, replica_groups=mesh['gx'=4,'gy_0'=2,'gy_1'=2,'gz_0'=4,'gz_1'=2] {'gz_0','gz_1'}, dimensions={0} | all-to-all | bytes 8388608 | tf_op jit(solution)/shard_map/all_to_all | solution.py:135
  (44 shorter events, 70.3 us)
Async XLA Ops:
  10.9 15.0 %collective-permute-start.1 = (f32[64,128,1]{1,0,2:T(8,128)S(1)}, f32[64,128,1]{1,0,2:T(8,128)S(1)}, u32[]{:S(2)}, u32[]{:S(2)}) collective-permute-start(f32[64,128,1]{1,0,2:T(8,128)S(1)} %copy.27), channel_id=1, source_target_pairs={{0,8},{8,16},{16,24},{24,0},{1,9},{9,17},{17,25},{25,1},{2,10},{10... | collective-permute-start | bytes 98312 | tf_op jit(solution)/shard_map/ppermute | solution.py:23
  13.8 16.7 %collective-permute-start.4 = (f32[64,128,1]{1,0,2:T(8,128)S(1)}, f32[64,128,1]{1,0,2:T(8,128)S(1)}, u32[]{:S(2)}, u32[]{:S(2)}) collective-permute-start(f32[64,128,1]{1,0,2:T(8,128)S(1)} %copy.28), channel_id=1, source_target_pairs={{8,0},{16,8},{24,16},{0,24},{9,1},{17,9},{25,17},{1,25},{10,2},{18... | collective-permute-start | bytes 98312 | tf_op jit(solution)/shard_map/ppermute | solution.py:24
  18.0 15.2 %collective-permute-start = (f32[1,128,128]{2,1,0:T(8,128)S(1)}, f32[1,128,128]{2,1,0:T(8,128)S(1)}, u32[]{:S(2)}, u32[]{:S(2)}) collective-permute-start(f32[1,128,128]{2,1,0:T(8,128)S(1)} %get-tuple-element.7), channel_id=1, source_target_pairs={{0,1},{1,2},{2,3},{3,4},{4,5},{5,6},{6,7},{7,0},{8,9},{9,10},{10,1... | collective-permute-start | bytes 196616 | tf_op jit(solution)/shard_map/ppermute | solution.py:23
  19.7 13.5 %collective-permute-start.5 = (f32[1,128,128]{2,1,0:T(8,128)S(1)}, f32[1,128,128]{2,1,0:T(8,128)S(1)}, u32[]{:S(2)}, u32[]{:S(2)}) collective-permute-start(f32[1,128,128]{2,1,0:T(8,128)S(1)} %get-tuple-element.8), channel_id=1, source_target_pairs={{1,0},{2,1},{3,2},{4,3},{5,4},{6,5},{7,6},{0,7},{9,8},{10,9},{11,1... | collective-permute-start | bytes 196616 | tf_op jit(solution)/shard_map/ppermute | solution.py:24
  24.3 8.8 %collective-permute-start.2 = (f32[64,1,128]{2,1,0:T(1,128)S(1)}, f32[64,1,128]{2,1,0:T(1,128)S(1)}, u32[]{:S(2)}, u32[]{:S(2)}) collective-permute-start(f32[64,1,128]{2,1,0:T(1,128)S(1)} %get-tuple-element.11), channel_id=1, source_target_pairs={{0,32},{32,64},{64,96},{96,0},{1,33},{33,65},{65,97},{97,1},{2,34}... | collective-permute-start | bytes 98312 | tf_op jit(solution)/shard_map/ppermute | solution.py:23
  25.9 7.2 %collective-permute-start.3 = (f32[64,1,128]{2,1,0:T(1,128)S(1)}, f32[64,1,128]{2,1,0:T(1,128)S(1)}, u32[]{:S(2)}, u32[]{:S(2)}) collective-permute-start(f32[64,1,128]{2,1,0:T(1,128)S(1)} %get-tuple-element.12), channel_id=1, source_target_pairs={{32,0},{64,32},{96,64},{0,96},{33,1},{65,33},{97,65},{1,97},{34,2}... | collective-permute-start | bytes 98312 | tf_op jit(solution)/shard_map/ppermute | solution.py:24
  48.9 34.8 %copy-start = (f32[66,130,130]{2,1,0:T(8,128)}, f32[66,130,130]{2,1,0:T(8,128)S(1)}, u32[]{:S(2)}) copy-start(f32[66,130,130]{2,1,0:T(8,128)S(1)} %get-tuple-element.5) | copy-start | bytes 13384804
  118.7 52.8 %all-to-all-start = ((f32[8,64,16,128]{3,2,1,0:T(8,128)}), f32[8,64,16,128]{3,2,1,0:T(8,128)}, u32[]{:S(2)}, u32[]{:S(2)}) async-start(f32[8,64,16,128]{3,2,1,0:T(8,128)} %fusion.66), calls=%async_computation | async-start | bytes 8388608 | tf_op jit(solution)/shard_map/all_to_all | solution.py:122
  201.3 84.4 %all-to-all-start.1 = ((f32[128,4,16,128]{3,2,1,0:T(8,128)}), f32[128,4,16,128]{3,2,1,0:T(8,128)}, u32[]{:S(2)}, u32[]{:S(2)}) async-start(f32[128,4,16,128]{3,2,1,0:T(8,128)} %copy.14), calls=%async_computation.1 | async-start | bytes 8388608 | tf_op jit(solution)/shard_map/all_to_all | solution.py:126
